TPU v7x, 512 devices: a whole 4x8x8 slice. The times are simulated.
512 devices in a mesh: gz: 32 (over y, x), gy: 16 (over z, core).
Axes of the slice: x: 4, y: 8, z: 8, core: 2. Of those that a mesh axis runs over, the one named last changes fastest.
Arguments:
- coarse_density: float32 [96, 96, 96], P(None, 'gy'), may hold values from -4 to 4
- density_in: float32 [192, 36864], P('gz', 'gy'), may hold values from -9 to 9
- history: float32 [8, 192, 36864], P(None, 'gz', 'gy'), may hold values from -12 to 12
- atom_cell: int32 [32, 16, 1], P('gz', 'gy'), may hold values from 0 to 13823
- atom_offset: float32 [3, 32, 16, 1], P(None, 'gz', 'gy'), may hold values from 0 to 1
- atom_charge: float32 [32, 16, 1], P('gz', 'gy'), may hold values from -16 to 16
- atom_width: float32 [32, 16, 1], P('gz', 'gy'), may hold values from 0.25 to 1
Outputs:
- residual: float32 [192, 36864], P('gz', 'gy')
- potential: float32 [192, 36864], P('gz', 'gy')
- intersections: float32 [9], replicated
Inputs may be any that keep to these rules, and one draw needn't show every extreme that they name: `atom_cell`: the cell lies inside the block of 6 x 12 x 192 fine cells of the slot's first two indices.
All inputs are finite; a program needn't handle non-finite values.
Results may differ from a plain program's by a relative error of at most 0.0003.
Values sent between devices are 32-bit elements; how exact they have to be, the bound alone decides.
A program may use at most 64 MiB of HBM per device.

v0:
```python
import functools

import jax
import jax.numpy as jnp
import numpy as np
from jax import lax
from jax.experimental import pallas as pl
from jax.experimental.pallas import tpu as pltpu
from jax.sharding import PartitionSpec as P

MESH = pl.DeviceIdType.MESH
NC = 96
NF = 192
HIST = 8
RC = 4
FZ = 6
FY = 12
NZ = 32
NY = 16
KX = NF // NY
KY = NF // NZ
STENCIL = ((-1, -1.0 / 16.0), (0, 9.0 / 16.0), (1, 9.0 / 16.0), (2, -1.0 / 16.0))
F32 = jnp.float32
BF16 = jnp.bfloat16


def two(table):
    high = np.asarray(table, np.float32).astype(jnp.bfloat16)
    low = (table - high.astype(np.float64)).astype(np.float32).astype(jnp.bfloat16)
    return high, low


def hartley():
    n = np.arange(NF)
    angle = 2.0 * np.pi / NF * (n[:, None] * n[None, :] % NF)
    return (np.cos(angle) + np.sin(angle)) / np.sqrt(NF)


def tables():
    h = hartley()
    rep = np.zeros((256, NY, 128))
    for j in range(NY):
        for g in range(9):
            rep[:NF, j, g * KX : (g + 1) * KX] = h[:, j * KX : (j + 1) * KX]
    rep = rep.reshape(256, NY * 128)
    by_y = h.reshape(NZ, KY, NY, FY)
    fy = np.zeros((NZ, 8, 2, NY, 8))
    fy[:, :KY, 0] = by_y[:, :, :, :8]
    fy[:, :KY, 1, :, :4] = by_y[:, :, :, 8:]
    fy[:, :KY, 1, :, 4:] = by_y[:, :, :, 8:]
    fy = fy.reshape(256, 256)
    fz = h.reshape(NF, NZ, FZ).transpose(0, 2, 1).reshape(NF, NF)
    ix = np.zeros((256, NC))
    for i in range(NC):
        ix[2 * i, i] = 1.0
        for offset, value in STENCIL:
            ix[2 * i + 1, (i + offset) % NC] += value
    wy = np.zeros((FY, FY // 2 + 3))
    for i in range(FY // 2):
        wy[2 * i, i + 1] = 1.0
        for offset, value in STENCIL:
            wy[2 * i + 1, i + 1 + offset] += value
    place = [(1, 5)] + [(0, r) for r in range(6)] + [(2, 0), (2, 1)]
    spread_y = np.zeros((72, 3, 6, 8))
    for z in range(FZ):
        for y in range(FY):
            row = 8 * z + y if y < 8 else 48 + 8 * (z % 3) + 4 * (z // 3) + y - 8
            for r, (block, coarse_y) in enumerate(place):
                spread_y[row, block, coarse_y, z] = wy[y, r]
    exact = [t.astype(np.float32).astype(jnp.bfloat16) for t in (ix.T, spread_y.reshape(72, 144))]
    return (*two(rep), *two(fy), *two(fy.T), *two(fz), *two(fz.T), *exact)


def split2(value):
    high = value.astype(BF16)
    return high, (value - high.astype(F32)).astype(BF16)


def split3(value):
    high = value.astype(BF16)
    rest = value - high.astype(F32)
    middle = rest.astype(BF16)
    return high, middle, (rest - middle.astype(F32)).astype(BF16)


def dot(a, b):
    return jnp.dot(a, b, preferred_element_type=F32)


def dot_nt(a, b):
    return lax.dot_general(a, b, (((1,), (1,)), ((), ())), preferred_element_type=F32)


def dot3(a, b, product=dot):
    return product(a[0], b[0]) + product(a[1], b[0]) + product(a[0], b[1])


def spread(t, count):
    return count // 2 + ((t + 1) // 2) * (1 - 2 * (t % 2))


def kernel(
    cell_in, offset_in, charge_in, width_in, coarse_in, density_in, history_in, *refs
):
    tables_in, refs = refs[:12], refs[12:]
    residual_out, potential_out, sums_out = refs[:3]
    (
        cell, offset, charge, width, coarse, density, history,
        rep_h, rep_l, fy_h, fy_l, gy_h, gy_l, fz_h, fz_l, gz_h, gz_l, ix, spread_y,
        planes, atoms, field_0, field_1, out_0, out_1, hist_0, hist_1,
        send1, recv1, send2, recv2, send4, recv4, send5, recv5, send_h, recv_h,
        weight, row_a, row_b,
        load_sem, halo_send, halo_recv, atom_send, atom_recv,
        s1, r1, s2, r2, s4, r4, s5, r5, sh, rh, sa, ra, sb, rb,
    ) = refs[3:]
    gz = lax.axis_index("gz")
    gy = lax.axis_index("gy")

    def zy(dz, dy):
        return ((gz + dz + NZ) % NZ, (gy + dy + NY) % NY)

    barrier = pltpu.get_barrier_semaphore()

    def greet_y(t, _):
        j = (gy + spread(t, NY)) % NY
        pl.semaphore_signal(barrier, inc=1, device_id=(gz, j), device_id_type=MESH)
        return 0

    def greet_z(t, _):
        j = (gz + spread(t, NZ)) % NZ
        pl.semaphore_signal(barrier, inc=1, device_id=(j, gy), device_id_type=MESH)
        return 0

    lax.fori_loop(0, NZ - 1, greet_z, 0)
    lax.fori_loop(0, NY - 1, greet_y, 0)
    for dz in (-1, 1):
        for dy in (-1, 1):
            pl.semaphore_signal(barrier, inc=1, device_id=zy(dz, dy), device_id_type=MESH)

    sources = (
        cell_in, offset_in, charge_in, width_in, coarse_in, density_in, tables_in[11], tables_in[10],
        tables_in[0], tables_in[1], tables_in[2], tables_in[3], history_in,
        *tables_in[4:10],
    )
    targets = (
        cell, offset, charge, width, coarse, density, spread_y, ix,
        rep_h, rep_l, fy_h, fy_l, history, gy_h, gy_l, fz_h, fz_l, gz_h, gz_l,
    )
    loads = {}
    for k, (source, target) in enumerate(zip(sources, targets)):
        loads[k] = pltpu.make_async_copy(source, target, load_sem.at[k])
        loads[k].start()

    row8 = lax.broadcasted_iota(jnp.int32, (8, 128), 0)
    lane8 = lax.broadcasted_iota(jnp.int32, (8, 128), 1)
    group = jnp.zeros_like(lane8)
    for c in range(1, 11):
        group = group + (lane8 >= c * KX).astype(jnp.int32)

    def square(counter):
        wave = jnp.where(counter < NF // 2, counter, counter - NF)
        return wave * wave

    wave_yx = (square(gz * KY + group) + square(gy * KX + lane8 - KX * group))[0:1]
    used = (lane8 < KY * KX)[0:1]
    squares = square(lax.broadcasted_iota(jnp.int32, (NF, 128), 0)) + wave_yx
    scaled = (2.0 * np.pi / NF) ** 2 * jnp.maximum(squares, 1).astype(F32)
    weight[...] = jnp.where((squares > 0) & used, 4.0 * np.pi / scaled, 0.0)

    for k in range(4):
        loads[k].wait()

    def whole_tile(value):
        return jnp.broadcast_to(value, (8, 128))

    site = whole_tile(cell[0].astype(F32))
    site_z = jnp.zeros((8, 128), F32)
    for k in range(1, FZ):
        site_z = site_z + (site >= float(k * FY * NF)).astype(F32)
    site = site - site_z * float(FY * NF)
    site_y = jnp.zeros((8, 128), F32)
    for k in range(1, FY):
        site_y = site_y + (site >= float(k * NF)).astype(F32)
    site_x = site - site_y * float(NF)
    own = whole_tile(width[0])
    offsets = offset[0, 0]
    for k, value in enumerate(
        (site_z, site_y, site_x, *(whole_tile(offsets[:, i : i + 1]) for i in range(3)), whole_tile(charge[0]))
    ):
        own = jnp.where(row8 == k, value, own)
    atoms[4] = own

    plane_of = lax.broadcasted_iota(jnp.int32, (8, NC), 1)
    fine_of = lax.broadcasted_iota(jnp.int32, (8, NC), 0)
    away = plane_of - gz * (FZ // 2) - fine_of // 2
    away = jnp.where(away < 0, away + NC, away)
    odd = jnp.zeros((8, NC), F32)
    for shift, value in STENCIL:
        odd = jnp.where(away == shift % NC, value, odd)
    even = jnp.where(away == 0, 1.0, 0.0)
    along_z = jnp.where(fine_of % 2 == 1, odd, even)
    along_z = jnp.where(fine_of < FZ, along_z, 0.0).astype(BF16)
    loads[4].wait()
    for k in range(6):
        parts = split3(coarse[k])
        planes[k] = dot(along_z, parts[0]) + dot(along_z, parts[1]) + dot(along_z, parts[2])

    pl.semaphore_wait(barrier, NY - 1 + NZ - 1 + 4)

    neighbours = []
    for dz in (-1, 1, 0):
        for dy in (-1, 1, 0):
            if (dz, dy) != (0, 0):
                slot = (1 - dz) * 3 + 1 - dy
                neighbours.append(
                    pltpu.make_async_remote_copy(
                        atoms.at[4], atoms.at[slot], atom_send.at[slot], atom_recv.at[slot],
                        device_id=zy(dz, dy), device_id_type=MESH,
                    )
                )
    own_planes = planes.at[pl.ds(0, 6)]
    halos = [
        pltpu.make_async_remote_copy(
            own_planes, planes.at[pl.ds(6 * k, 6)], halo_send.at[k - 1], halo_recv.at[k - 1],
            device_id=zy(0, dy), device_id_type=MESH,
        )
        for k, dy in ((1, 1), (2, -1))
    ]
    for copy in neighbours:
        copy.start()
    for copy in halos:
        copy.start()

    lane128 = lax.broadcasted_iota(jnp.int32, (FZ, 128), 1)
    loads[5].wait()

    def put(y, low, high):
        if y < 8:
            field_0[pl.ds(y, FZ, stride=8), :] = low
            field_1[pl.ds(y, FZ, stride=8), :] = high
        else:
            for half in range(2):
                rows = pl.ds(40 + y + 4 * half, 3, stride=8)
                field_0[rows, :] = low[3 * half : 3 * half + 3]
                field_1[rows, :] = high[3 * half : 3 * half + 3]

    for pair in range(FY // 2):
        a, b, c = (density[:, 384 * pair + 128 * k : 384 * pair + 128 * k + 128] for k in range(3))
        rolled_b = pltpu.roll(b, 64, 1)
        rolled_c = pltpu.roll(c, 64, 1)
        put(2 * pair, a, b)
        put(2 * pair + 1, jnp.where(lane128 < 64, rolled_b, rolled_c), rolled_c)

    x = lax.broadcasted_iota(jnp.int32, (1, 256), 1).astype(F32)
    y_low = row8.astype(F32)
    y_high = jnp.where(row8 < 4, row8 + 8, row8 + 4).astype(F32)
    z = row8.astype(F32)

    def double(value):
        return jnp.concatenate([value, value], axis=1)

    upper = double(row8) < 4

    def charge_of(k):
        tile = atoms[k]
        dz, dy = k // 3 - 1, k % 3 - 1
        exponent = tile[7:8]
        wide = double(tile)
        from_z = (z - float(FZ * dz) - tile[0:1]) - tile[3:4]
        from_low = (y_low - float(FY * dy) - tile[1:2]) - tile[4:5]
        from_high = (y_high - float(FY * dy) - tile[1:2]) - tile[4:5]
        from_x = x - wide[2:3]
        from_x = jnp.where(from_x >= NF / 2, from_x - NF, from_x)
        from_x = jnp.where(from_x < -NF / 2, from_x + NF, from_x)
        from_x = from_x - wide[5:6]
        exp_z = double(jnp.exp(-exponent * (from_z * from_z)))
        exp_x = jnp.exp(-wide[7:8] * (from_x * from_x))
        low = double(jnp.exp(-exponent * (from_low * from_low))) * exp_x
        high = double(jnp.exp(-exponent * (from_high * from_high))) * exp_x
        floor = jnp.exp(-wide[7:8] * float(RC * RC))
        ratio = wide[7:8] / np.pi
        factor = wide[6:7] * (ratio * jnp.sqrt(ratio))
        powers = [low * exp_z[c : c + 1] for c in range(FZ)]
        powers += [high * jnp.where(upper, exp_z[c : c + 1], exp_z[c + 3 : c + 4]) for c in range(3)]
        return [factor * jnp.maximum(power - floor, 0.0) for power in powers]

    total = charge_of(4)
    for k in range(6, 12):
        loads[k].wait()
    for copy in neighbours:
        copy.wait_recv()
    for k in range(9):
        if k != 4:
            total = [a + b for a, b in zip(total, charge_of(k))]

    for copy in halos:
        copy.wait_recv()
    parts = split3(planes[...].reshape(144, NC))
    table = ix[...]
    along_x = dot(parts[0], table) + dot(parts[1], table) + dot(parts[2], table)
    parts = split3(along_x)
    table = spread_y[...]
    smooth = dot(table, parts[0]) + dot(table, parts[1]) + dot(table, parts[2])

    inside = lax.broadcasted_iota(jnp.int32, (8, 256), 1) < NF
    blocks = []
    for g in range(9):
        rows = slice(8 * g, 8 * g + 8)
        given = jnp.concatenate([field_0[rows, :], field_1[rows, :]], axis=1)
        value = jnp.where(inside, smooth[rows] + total[g] - given, 0.0)
        blocks.append(value)
        field_0[rows, :] = value[:, :128]
        field_1[rows, :] = value[:, 128:]

    group256 = double(group)

    def along_x_forward(values, store):
        halves = split2(values)
        for p in range(NY // 2):
            span = slice(256 * p, 256 * p + 256)
            out = dot3(halves, (rep_h[:, span], rep_l[:, span]))
            chosen = out[0:8]
            for g in range(1, 9):
                chosen = jnp.where(group256 >= g, out[8 * g : 8 * g + 8], chosen)
            store(2 * p, chosen[:, :128])
            store(2 * p + 1, chosen[:, 128:])

    def exchange_y(send, recv, ssem, rsem):
        def body(t, _):
            j = (gy + spread(t, NY)) % NY
            pltpu.make_async_remote_copy(
                send.at[j], recv.at[gy], ssem, rsem, device_id=(gz, j), device_id_type=MESH
            ).start()
            return 0

        lax.fori_loop(0, NY - 1, body, 0)
        recv[gy] = send[gy]
        whole = recv.at[pl.ds(0, NY - 1)]
        return pltpu.make_async_copy(whole, whole, rsem), pltpu.make_async_copy(whole, whole, ssem)

    def exchange_z(send, recv, ssem, rsem):
        mine = pl.ds(pl.multiple_of(gz * 8, 8), KY)

        def body(t, _):
            j = (gz + spread(t, NZ)) % NZ
            pltpu.make_async_remote_copy(
                send.at[pl.ds(pl.multiple_of(j * 8, 8), KY)], recv.at[mine],
                ssem, rsem, device_id=(j, gy), device_id_type=MESH,
            ).start()
            return 0

        lax.fori_loop(0, NZ - 1, body, 0)
        recv[mine, :] = send[mine, :]
        whole = recv.at[pl.ds(0, KY * (NZ - 1))]
        return pltpu.make_async_copy(whole, whole, rsem), pltpu.make_async_copy(whole, whole, ssem)

    def store_residual(j, value):
        send1[j] = value

    along_x_forward(jnp.concatenate(blocks, axis=0), store_residual)
    arrived, sent1 = exchange_y(send1, recv1, s1, r1)

    loads[12].wait()
    lane_h = lax.broadcasted_iota(jnp.int32, (HIST, 128), 1)
    for c in range(FZ):
        for pair in range(FY // 2):
            a, b, d = (history[c, :, 384 * pair + 128 * k : 384 * pair + 128 * k + 128] for k in range(3))
            rolled_b = pltpu.roll(b, 64, 1)
            rolled_d = pltpu.roll(d, 64, 1)
            for y, low, high in (
                (2 * pair, a, jnp.where(lane_h < 64, b, 0.0)),
                (2 * pair + 1, jnp.where(lane_h < 64, rolled_b, rolled_d), jnp.where(lane_h < 64, rolled_d, 0.0)),
            ):
                row = 8 * c + y if y < 8 else 48 + 8 * (c % 3) + 4 * (c // 3) + y - 8
                hist_0[pl.ds(row, HIST, stride=72), :] = low
                hist_1[pl.ds(row, HIST, stride=72), :] = high

    def one_history(i, _):
        rows = pl.ds(pl.multiple_of(i * 72, 8), 72)

        def store(j, value):
            send_h[j, i] = value

        along_x_forward(jnp.concatenate([hist_0[rows, :], hist_1[rows, :]], axis=1), store)
        return 0

    lax.fori_loop(0, HIST, one_history, 0)

    groups128 = jnp.concatenate([group] * NY, axis=0)
    rows128 = jnp.concatenate([row8] * NY, axis=0)
    from_upper = (groups128 < 3) & (rows128 < 4)
    from_lower = (groups128 >= 3) & (groups128 < 6) & (rows128 >= 4)
    arrived.wait()
    packed = recv1[...].reshape(128, 128)
    moved = jnp.where(
        from_upper, pltpu.roll(packed, 128 - 72, 1), jnp.where(from_lower, pltpu.roll(packed, 128 - 36, 1), 0.0)
    )
    send2[...] = dot3((fy_h[...], fy_l[...]), split2(jnp.concatenate([packed, moved], axis=0)))
    arrived, sent2 = exchange_z(send2, recv2, s2, r2)
    arrived_h, sent_h = exchange_y(send_h, recv_h, sh, rh)

    def give(out, first, second):
        for pair in range(FY // 2):
            if pair < 4:
                places = ((0, FZ, 2 * pair),)
            else:
                places = ((0, 3, 40 + 2 * pair), (3, 3, 44 + 2 * pair))
            for top, count, row in places:
                low_lanes = lax.broadcasted_iota(jnp.int32, (count, 128), 1) < 64
                a = first[pl.ds(row, count, stride=8), :]
                b = second[pl.ds(row, count, stride=8), :]
                c = pltpu.roll(first[pl.ds(row + 1, count, stride=8), :], 64, 1)
                d = pltpu.roll(second[pl.ds(row + 1, count, stride=8), :], 64, 1)
                tiles = (a, jnp.where(low_lanes, b, c), jnp.where(low_lanes, c, d))
                for k, tile in enumerate(tiles):
                    out[top : top + count, 384 * pair + 128 * k : 384 * pair + 128 * k + 128] = tile

    give(residual_out, field_0, field_1)
    for k in range(13, 19):
        loads[k].wait()
    arrived.wait()

    group1 = group[0:1]

    def swapped(pieces, position):
        result = None
        for b in range(6):
            shift = (KX * (b - position)) % 128
            moved = pltpu.roll(pieces[b], shift, 1) if shift else pieces[b]
            result = moved if result is None else jnp.where(group1 >= b, moved, result)
        return result

    pieces = [recv2[pl.ds(b, NZ, stride=8), :] for b in range(KY)]
    stacked = jnp.concatenate([swapped(pieces, a) for a in range(FZ)], axis=0)
    spectrum = dot3((fz_h[...], fz_l[...]), split2(stacked)) * weight[...]
    back = dot3((gz_h[...], gz_l[...]), split2(spectrum))
    pieces = [back[NZ * a : NZ * a + NZ] for a in range(FZ)]
    for b in range(KY):
        send4[pl.ds(b, NZ, stride=8), :] = swapped(pieces, b)
    arrived, sent4 = exchange_z(send4, recv4, s4, r4)
    arrived.wait()

    rows256 = jnp.concatenate([rows128, rows128], axis=0)
    out = dot3((gy_h[...], gy_l[...]), split2(jnp.where(rows256 < KY, recv4[0:256, :], 0.0)))
    low, high = out[:128], out[128:]
    packed = jnp.where(
        groups128 < 6, low, jnp.where(rows128 < 4, pltpu.roll(high, 72, 1), pltpu.roll(high, 36, 1))
    )
    for j in range(NY):
        send5[j] = packed[8 * j : 8 * j + 8]
    arrived, sent5 = exchange_y(send5, recv5, s5, r5)

    arrived_h.wait()
    terms = [jnp.zeros((8, 128), F32) for _ in range(HIST + 1)]
    for j in range(NY):
        tile = jnp.where(group < 9, packed[8 * j : 8 * j + 8], 0.0)
        for i in range(HIST):
            terms[i] = terms[i] + recv_h[j, i] * tile
        terms[HIST] = terms[HIST] + recv1[j] * tile
    rows = jnp.concatenate(
        [jnp.sum(t, axis=0, keepdims=True) for t in terms] + [jnp.zeros((7, 128), F32)], axis=0
    ) * (1.0 / float(NF) ** 3)
    column = jnp.sum(rows, axis=1, keepdims=True)
    lane_of = lax.broadcasted_iota(jnp.int32, (16, 128), 1)
    row_of = lax.broadcasted_iota(jnp.int32, (16, 128), 0)
    line = jnp.sum(jnp.where(lane_of == row_of, column, 0.0), axis=0, keepdims=True)

    row_b[gz] = line

    def body_b(t, _):
        j = (gz + spread(t, NZ)) % NZ
        pltpu.make_async_remote_copy(
            row_b.at[gz], row_b.at[gz], sb, rb, device_id=(j, gy), device_id_type=MESH
        ).start()
        return 0

    lax.fori_loop(0, NZ - 1, body_b, 0)
    whole_b = row_b.at[pl.ds(0, NZ - 1)]
    pltpu.make_async_copy(whole_b, whole_b, rb).wait()
    row_a[gy] = jnp.sum(row_b[...], axis=0)

    def body_a(t, _):
        j = (gy + spread(t, NY)) % NY
        pltpu.make_async_remote_copy(
            row_a.at[gy], row_a.at[gy], sa, ra, device_id=(gz, j), device_id_type=MESH
        ).start()
        return 0

    lax.fori_loop(0, NY - 1, body_a, 0)

    arrived.wait()
    potential = jnp.zeros((72, 256), F32)
    for p in range(NY // 2):
        pair = split2(jnp.concatenate([recv5[2 * p], recv5[2 * p + 1]], axis=1))
        masked = [
            jnp.concatenate([jnp.where(group256 == g, part.astype(F32), 0.0) for g in range(9)], axis=0).astype(BF16)
            for part in pair
        ]
        span = slice(256 * p, 256 * p + 256)
        potential = potential + dot3(masked, (rep_h[:, span], rep_l[:, span]), dot_nt)
    out_0[0:72, :] = potential[:, :128]
    out_1[0:72, :] = potential[:, 128:]
    give(potential_out, out_0, out_1)

    whole_a = row_a.at[pl.ds(0, NY - 1)]
    pltpu.make_async_copy(whole_a, whole_a, ra).wait()
    sums_out[...] = jnp.sum(row_a[...], axis=0)

    for copy in neighbours:
        copy.wait_send()
    for copy in halos:
        copy.wait_send()
    for copy in (sent1, sent2, sent_h, sent4, sent5):
        copy.wait()
    pltpu.make_async_copy(whole_a, whole_a, sa).wait()
    pltpu.make_async_copy(whole_b, whole_b, sb).wait()


def solution(mesh):
    constants = tables()

    def local(coarse, density, history, cell, offset, charge, width):
        coarse = jnp.transpose(coarse, (1, 0, 2))
        history = jnp.transpose(history, (1, 0, 2))
        offset = jnp.transpose(offset, (1, 2, 3, 0))
        inputs = (cell, offset, charge, width, coarse, density, history)
        inputs = inputs + tuple(jnp.asarray(c) for c in constants)
        vmem = pl.BlockSpec(memory_space=pltpu.VMEM)
        dma = pltpu.SemaphoreType.DMA
        tile = (NY, 8, 128)
        residual, potential, sums = pl.pallas_call(
            kernel,
            out_shape=(
                jax.ShapeDtypeStruct((FZ, FY * NF), F32),
                jax.ShapeDtypeStruct((FZ, FY * NF), F32),
                jax.ShapeDtypeStruct((1, 128), F32),
            ),
            in_specs=[pl.BlockSpec(memory_space=pl.ANY)] * len(inputs),
            out_specs=(vmem, vmem, vmem),
            scratch_shapes=[
                *(pltpu.VMEM(i.shape, i.dtype) for i in inputs),
                pltpu.VMEM((18, 8, NC), F32),
                pltpu.VMEM((9, 8, 128), F32),
                *[pltpu.VMEM((128, 128), F32)] * 4,
                *[pltpu.VMEM((648, 128), F32)] * 2,
                *[pltpu.VMEM(tile, F32)] * 2,
                pltpu.VMEM((256, 128), F32),
                *[pltpu.VMEM((264, 128), F32)] * 3,
                *[pltpu.VMEM(tile, F32)] * 2,
                *[pltpu.VMEM((NY, HIST, 8, 128), F32)] * 2,
                pltpu.VMEM((NF, 128), F32),
                pltpu.VMEM((NY, 1, 128), F32),
                pltpu.VMEM((NZ, 1, 128), F32),
                dma((19,)), dma((2,)), dma((2,)), dma((9,)), dma((9,)),
                *[dma] * 14,
            ],
            compiler_params=pltpu.CompilerParams(collective_id=0, has_side_effects=True),
        )(*inputs)
        return residual, potential, sums[0, : HIST + 1]

    in_specs = (
        P(None, "gy", None),
        P("gz", "gy"),
        P(None, "gz", "gy"),
        P("gz", "gy", None),
        P(None, "gz", "gy", None),
        P("gz", "gy", None),
        P("gz", "gy", None),
    )
    out_specs = (P("gz", "gy"), P("gz", "gy"), P())
    return jax.shard_map(local, mesh=mesh, in_specs=in_specs, out_specs=out_specs, check_vma=False)
```

profile of v0, /device:TPU:1, one launch (start us, length us, event | category | flops | bytes accessed | tf_op | source)
XLA Modules:
  0.0 59.6 jit_solution(13682777322067366575)
XLA Ops:
  2.6 53.7 %shard_map.202 = (f32[6,2304]{1,0:T(8,128)}, f32[6,2304]{1,0:T(8,128)}, f32[1,128]{1,0:T(1,128)}) custom-call(s32[1,1,1]{2,1,0:T(1,128)S(6)} %copy.24.cell_in, f32[1,1,1,3]{3,2,1,0:T(1,128)} %bitcast.7, f32[1,1,1]{2,1,0:T(1,128)S(6)} %copy.25.charge_in, f32[1,1,1]{2,1,0:T(1,128)S(6)} %copy.26.width_in, f32[6,96,96]{2,1,0:T(8,128)} %bitcast.6, ...), custom_call_target="tpu_custom_call" | custom-call | tf_op jit(solution)/shard_map/pallas_call | solution.py:531
  56.3 0.0 copy-start.1
  56.3 0.6 %copy-done.1 = f32[1,128]{1,0:T(1,128)S(1)} copy-done((f32[1,128]{1,0:T(1,128)S(1)}, f32[1,128]{1,0:T(1,128)}, u32[]{:S(2)}) %copy-start.1) | copy-done | bytes 536
  56.9 0.5 slice_bitcast_fusion
  57.4 0.0 copy-start
  57.4 1.6 %copy.27 = f32[6,2304]{1,0:T(8,128)} copy(f32[6,2304]{1,0:T(8,128)} %get-tuple-element.12) | data formatting | bytes 110592
  59.0 0.0 copy-done
  59.0 0.6 %copy.28 = f32[6,2304]{1,0:T(8,128)} copy(f32[6,2304]{1,0:T(8,128)S(1)} %copy-done) | data formatting | bytes 110592
Async XLA Ops:
  56.3 0.6 %copy-start.1 = (f32[1,128]{1,0:T(1,128)S(1)}, f32[1,128]{1,0:T(1,128)}, u32[]{:S(2)}) copy-start(f32[1,128]{1,0:T(1,128)} %get-tuple-element.8) | copy-start | bytes 1540
  57.4 1.6 %copy-start = (f32[6,2304]{1,0:T(8,128)S(1)}, f32[6,2304]{1,0:T(8,128)}, u32[]{:S(2)}) copy-start(f32[6,2304]{1,0:T(8,128)} %get-tuple-element.13) | copy-start | bytes 165892
where the time goes:
time: 59.8 us; the launch traced here: 59.6 us
  Pallas kernels  53.7 us (90%)
  local copies, waits for them, and re-layouts  3.31 us (6%)
  between operations  2.59 us (4%)
    pallas_call x1, Pallas kernels, local(): pl.pallas_call(kernel, out_shape=(jax.ShapeDtypeStruct((FZ, FY * NF), F32...  53.7 us
    unnamed x6, local copies, waits for them, and re-layouts  2.8 us

commit v1 on v0

--- a/solution.py
+++ b/solution.py
@@ -95,8 +95,19 @@
     return product(a[0], b[0]) + product(a[1], b[0]) + product(a[0], b[1])
 
 
-def spread(t, count):
-    return count // 2 + ((t + 1) // 2) * (1 - 2 * (t % 2))
+def wrap(index, count):
+    return jnp.where(index >= count, index - count, index)
+
+
+def each_partner(me, count, act):
+    act(wrap(me + count // 2, count))
+
+    def body(t, _):
+        act(wrap(me + count // 2 - t, count))
+        act(wrap(me + count // 2 + t, count))
+        return 0
+
+    lax.fori_loop(1, count // 2, body, 0, unroll=True)
 
 
 def kernel(
@@ -111,31 +122,28 @@
         send1, recv1, send2, recv2, send4, recv4, send5, recv5, send_h, recv_h,
         weight, row_a, row_b,
         load_sem, halo_send, halo_recv, atom_send, atom_recv,
-        s1, r1, s2, r2, s4, r4, s5, r5, sh, rh, sa, ra, sb, rb,
+        s1, r1, s2, r2, s4, r4, s5, r5, sh, rh, sa, ra, sb, rb, ring_z_ready, ring_y_ready, plane_ready,
     ) = refs[3:]
     gz = lax.axis_index("gz")
     gy = lax.axis_index("gy")
 
     def zy(dz, dy):
-        return ((gz + dz + NZ) % NZ, (gy + dy + NY) % NY)
+        return (wrap(wrap(gz + dz + NZ, NZ), NZ) if dz else gz, wrap(wrap(gy + dy + NY, NY), NY) if dy else gy)
 
     barrier = pltpu.get_barrier_semaphore()
 
-    def greet_y(t, _):
-        j = (gy + spread(t, NY)) % NY
-        pl.semaphore_signal(barrier, inc=1, device_id=(gz, j), device_id_type=MESH)
-        return 0
-
-    def greet_z(t, _):
-        j = (gz + spread(t, NZ)) % NZ
-        pl.semaphore_signal(barrier, inc=1, device_id=(j, gy), device_id_type=MESH)
-        return 0
-
-    lax.fori_loop(0, NZ - 1, greet_z, 0)
-    lax.fori_loop(0, NY - 1, greet_y, 0)
-    for dz in (-1, 1):
-        for dy in (-1, 1):
-            pl.semaphore_signal(barrier, inc=1, device_id=zy(dz, dy), device_id_type=MESH)
+    def greet(semaphore, z, y):
+        pl.semaphore_signal(semaphore, inc=1, device_id=(z, y), device_id_type=MESH)
+
+    column = lax.rem(gz, 4)
+    ring_x = [gz - column + lax.rem(column + k, 4) for k in (2, 1, 3)]
+    other_core = gy + 1 - 2 * lax.rem(gy, 2)
+    greeted = [zy(dz, dy) for dz in (-1, 1) for dy in (-1, 1)]
+    greeted += [zy(dz, 0) for dz in (-8, 8)] + [(j, gy) for j in ring_x]
+    greeted += [(gz, wrap(wrap(core + dy + NY, NY), NY)) for dy in (-4, 4, -2, 2) for core in (gy, other_core)]
+    greeted += [zy(dz, 0) for dz in (-4, 4, -1, 1)] + [(gz, other_core)]
+    for z, y in greeted:
+        greet(barrier, z, y)
 
     sources = (
         cell_in, offset_in, charge_in, width_in, coarse_in, density_in, tables_in[11], tables_in[10],
@@ -205,18 +213,16 @@
         parts = split3(coarse[k])
         planes[k] = dot(along_z, parts[0]) + dot(along_z, parts[1]) + dot(along_z, parts[2])
 
-    pl.semaphore_wait(barrier, NY - 1 + NZ - 1 + 4)
-
-    neighbours = []
+    pl.semaphore_wait(barrier, len(greeted))
+
+    neighbours = {}
     for dz in (-1, 1, 0):
         for dy in (-1, 1, 0):
             if (dz, dy) != (0, 0):
                 slot = (1 - dz) * 3 + 1 - dy
-                neighbours.append(
-                    pltpu.make_async_remote_copy(
-                        atoms.at[4], atoms.at[slot], atom_send.at[slot], atom_recv.at[slot],
-                        device_id=zy(dz, dy), device_id_type=MESH,
-                    )
+                neighbours[slot] = pltpu.make_async_remote_copy(
+                    atoms.at[4], atoms.at[slot], atom_send.at[slot], atom_recv.at[slot],
+                    device_id=zy(dz, dy), device_id_type=MESH,
                 )
     own_planes = planes.at[pl.ds(0, 6)]
     halos = [
@@ -226,10 +232,14 @@
         )
         for k, dy in ((1, 1), (2, -1))
     ]
-    for copy in neighbours:
+    for copy in neighbours.values():
         copy.start()
     for copy in halos:
         copy.start()
+    for dy in (-4, 4):
+        greet(ring_z_ready, *zy(0, dy))
+    for dz in (-8, 8):
+        greet(ring_y_ready, *zy(dz, 0))
 
     lane128 = lax.broadcasted_iota(jnp.int32, (FZ, 128), 1)
     loads[5].wait()
@@ -287,11 +297,6 @@
     total = charge_of(4)
     for k in range(6, 12):
         loads[k].wait()
-    for copy in neighbours:
-        copy.wait_recv()
-    for k in range(9):
-        if k != 4:
-            total = [a + b for a, b in zip(total, charge_of(k))]
 
     for copy in halos:
         copy.wait_recv()
@@ -301,6 +306,10 @@
     parts = split3(along_x)
     table = spread_y[...]
     smooth = dot(table, parts[0]) + dot(table, parts[1]) + dot(table, parts[2])
+
+    for k in (3, 5, 1, 7, 0, 2, 6, 8):
+        neighbours[k].wait_recv()
+        total = [a + b for a, b in zip(total, charge_of(k))]
 
     inside = lax.broadcasted_iota(jnp.int32, (8, 256), 1) < NF
     blocks = []
@@ -326,14 +335,12 @@
             store(2 * p + 1, chosen[:, 128:])
 
     def exchange_y(send, recv, ssem, rsem):
-        def body(t, _):
-            j = (gy + spread(t, NY)) % NY
+        def act(j):
             pltpu.make_async_remote_copy(
                 send.at[j], recv.at[gy], ssem, rsem, device_id=(gz, j), device_id_type=MESH
             ).start()
-            return 0
-
-        lax.fori_loop(0, NY - 1, body, 0)
+
+        each_partner(gy, NY, act)
         recv[gy] = send[gy]
         whole = recv.at[pl.ds(0, NY - 1)]
         return pltpu.make_async_copy(whole, whole, rsem), pltpu.make_async_copy(whole, whole, ssem)
@@ -341,15 +348,13 @@
     def exchange_z(send, recv, ssem, rsem):
         mine = pl.ds(pl.multiple_of(gz * 8, 8), KY)
 
-        def body(t, _):
-            j = (gz + spread(t, NZ)) % NZ
+        def act(j):
             pltpu.make_async_remote_copy(
                 send.at[pl.ds(pl.multiple_of(j * 8, 8), KY)], recv.at[mine],
                 ssem, rsem, device_id=(j, gy), device_id_type=MESH,
             ).start()
-            return 0
-
-        lax.fori_loop(0, NZ - 1, body, 0)
+
+        each_partner(gz, NZ, act)
         recv[mine, :] = send[mine, :]
         whole = recv.at[pl.ds(0, KY * (NZ - 1))]
         return pltpu.make_async_copy(whole, whole, rsem), pltpu.make_async_copy(whole, whole, ssem)
@@ -358,7 +363,12 @@
         send1[j] = value
 
     along_x_forward(jnp.concatenate(blocks, axis=0), store_residual)
+    pl.semaphore_wait(ring_z_ready, 2)
     arrived, sent1 = exchange_y(send1, recv1, s1, r1)
+
+    pl.semaphore_wait(ring_y_ready, 2)
+    for j in ring_x:
+        greet(plane_ready, j, gy)
 
     loads[12].wait()
     lane_h = lax.broadcasted_iota(jnp.int32, (HIST, 128), 1)
@@ -396,6 +406,7 @@
         from_upper, pltpu.roll(packed, 128 - 72, 1), jnp.where(from_lower, pltpu.roll(packed, 128 - 36, 1), 0.0)
     )
     send2[...] = dot3((fy_h[...], fy_l[...]), split2(jnp.concatenate([packed, moved], axis=0)))
+    pl.semaphore_wait(plane_ready, 3)
     arrived, sent2 = exchange_z(send2, recv2, s2, r2)
     arrived_h, sent_h = exchange_y(send_h, recv_h, sh, rh)
 
@@ -446,10 +457,6 @@
     packed = jnp.where(
         groups128 < 6, low, jnp.where(rows128 < 4, pltpu.roll(high, 72, 1), pltpu.roll(high, 36, 1))
     )
-    for j in range(NY):
-        send5[j] = packed[8 * j : 8 * j + 8]
-    arrived, sent5 = exchange_y(send5, recv5, s5, r5)
-
     arrived_h.wait()
     terms = [jnp.zeros((8, 128), F32) for _ in range(HIST + 1)]
     for j in range(NY):
@@ -467,26 +474,25 @@
 
     row_b[gz] = line
 
-    def body_b(t, _):
-        j = (gz + spread(t, NZ)) % NZ
+    def act_b(j):
         pltpu.make_async_remote_copy(
             row_b.at[gz], row_b.at[gz], sb, rb, device_id=(j, gy), device_id_type=MESH
         ).start()
-        return 0
-
-    lax.fori_loop(0, NZ - 1, body_b, 0)
+
+    each_partner(gz, NZ, act_b)
+    for j in range(NY):
+        send5[j] = packed[8 * j : 8 * j + 8]
+    arrived, sent5 = exchange_y(send5, recv5, s5, r5)
     whole_b = row_b.at[pl.ds(0, NZ - 1)]
     pltpu.make_async_copy(whole_b, whole_b, rb).wait()
     row_a[gy] = jnp.sum(row_b[...], axis=0)
 
-    def body_a(t, _):
-        j = (gy + spread(t, NY)) % NY
+    def act_a(j):
         pltpu.make_async_remote_copy(
             row_a.at[gy], row_a.at[gy], sa, ra, device_id=(gz, j), device_id_type=MESH
         ).start()
-        return 0
-
-    lax.fori_loop(0, NY - 1, body_a, 0)
+
+    each_partner(gy, NY, act_a)
 
     arrived.wait()
     potential = jnp.zeros((72, 256), F32)
@@ -504,9 +510,9 @@
 
     whole_a = row_a.at[pl.ds(0, NY - 1)]
     pltpu.make_async_copy(whole_a, whole_a, ra).wait()
-    sums_out[...] = jnp.sum(row_a[...], axis=0)
-
-    for copy in neighbours:
+    sums_out[...] = jnp.sum(row_a[...], axis=0)[0, : HIST + 1]
+
+    for copy in neighbours.values():
         copy.wait_send()
     for copy in halos:
         copy.wait_send()
@@ -514,6 +520,14 @@
         copy.wait()
     pltpu.make_async_copy(whole_a, whole_a, sa).wait()
     pltpu.make_async_copy(whole_b, whole_b, sb).wait()
+
+
+def write_out(*refs):
+    copies = [pltpu.make_async_copy(refs[k], refs[3 + k], refs[6].at[k]) for k in range(3)]
+    for copy in copies:
+        copy.start()
+    for copy in copies:
+        copy.wait()
 
 
 def solution(mesh):
@@ -531,11 +545,11 @@
         residual, potential, sums = pl.pallas_call(
             kernel,
             out_shape=(
-                jax.ShapeDtypeStruct((FZ, FY * NF), F32),
-                jax.ShapeDtypeStruct((FZ, FY * NF), F32),
-                jax.ShapeDtypeStruct((1, 128), F32),
+                pltpu.VMEM((FZ, FY * NF), F32),
+                pltpu.VMEM((FZ, FY * NF), F32),
+                pltpu.VMEM((HIST + 1,), F32),
             ),
-            in_specs=[pl.BlockSpec(memory_space=pl.ANY)] * len(inputs),
+            in_specs=[pl.BlockSpec(memory_space=pltpu.HBM)] * len(inputs),
             out_specs=(vmem, vmem, vmem),
             scratch_shapes=[
                 *(pltpu.VMEM(i.shape, i.dtype) for i in inputs),
@@ -553,10 +567,19 @@
                 pltpu.VMEM((NZ, 1, 128), F32),
                 dma((19,)), dma((2,)), dma((2,)), dma((9,)), dma((9,)),
                 *[dma] * 14,
+                *[pltpu.SemaphoreType.REGULAR] * 3,
             ],
             compiler_params=pltpu.CompilerParams(collective_id=0, has_side_effects=True),
         )(*inputs)
-        return residual, potential, sums[0, : HIST + 1]
+        results = tuple(pltpu.with_memory_space_constraint(r, pltpu.VMEM) for r in (residual, potential, sums))
+        hbm = pl.BlockSpec(memory_space=pltpu.HBM)
+        return pl.pallas_call(
+            write_out,
+            out_shape=tuple(jax.ShapeDtypeStruct(r.shape, F32) for r in results),
+            in_specs=[vmem] * 3,
+            out_specs=(hbm,) * 3,
+            scratch_shapes=[dma((3,))],
+        )(*results)
 
     in_specs = (
         P(None, "gy", None),

time: 59.8 us -> 53.3 us (0.89)
  local copies, waits for them, and re-layouts: 3.31 us -> 0 us
  Pallas kernels: 53.7 us -> 50.6 us
    pallas_call x1 -> x2, Pallas kernels: 53.7 us -> 50.6 us  [the longest x1 49.9 us: local(): pl.pallas_call(kernel, out_shape=(pltpu.VMEM((FZ, FY * NF), F32), pltpu.V...]
    unnamed x6 -> x0, local copies, waits for them, and re-layouts: 2.8 us -> none
where the time goes in v1:
time: 53.3 us; the launch traced here: 53.2 us
  Pallas kernels  50.6 us (95%)
  between operations  2.58 us (5%)
    pallas_call x1, Pallas kernels, local(): pl.pallas_call(kernel, out_shape=(pltpu.VMEM((FZ, FY * NF), F32), pltpu.V...  49.9 us

profile of v1, /device:TPU:1, one launch (start us, length us, event | category | flops | bytes accessed | tf_op | source)
XLA Modules:
  0.0 53.2 jit_solution(17913584134702839297)
XLA Ops:
  2.6 49.9 %shard_map.202 = (f32[6,2304]{1,0:T(8,128)S(1)}, f32[6,2304]{1,0:T(8,128)S(1)}, f32[9]{0:T(128)S(1)}) custom-call(s32[1,1,1]{2,1,0:T(1,128)S(6)} %copy.22.cell_in, f32[1,1,1,3]{3,2,1,0:T(1,128)} %bitcast.5, f32[1,1,1]{2,1,0:T(1,128)S(6)} %copy.23.charge_in, f32[1,1,1]{2,1,0:T(1,128)S(6)} %copy.24.width_in, f32[6,96,96]{2,1,0:T(8,128)} %bitcast.4, ...), custom_call_target="tpu_custom_call" | custom-call | tf_op jit(solution)/shard_map/pallas_call | solution.py:545
  52.5 0.7 %shard_map.203 = (f32[6,2304]{1,0:T(8,128)}, f32[6,2304]{1,0:T(8,128)}, f32[9]{0:T(128)}) custom-call(f32[6,2304]{1,0:T(8,128)S(1)} %get-tuple-element.6.refs_0_, f32[6,2304]{1,0:T(8,128)S(1)} %get-tuple-element.7.refs_1_, f32[9]{0:T(128)S(1)} %get-tuple-element.8.refs_2_), custom_call_target="tpu_custom_call" | custom-call | tf_op jit(solution)/shard_map/pallas_call | solution.py:576

commit v2 on v1

--- a/solution.py
+++ b/solution.py
@@ -12,6 +12,7 @@
 NC = 96
 NF = 192
 HIST = 8
+EARLY = 3
 RC = 4
 FZ = 6
 FY = 12
@@ -68,7 +69,18 @@
             for r, (block, coarse_y) in enumerate(place):
                 spread_y[row, block, coarse_y, z] = wy[y, r]
     exact = [t.astype(np.float32).astype(jnp.bfloat16) for t in (ix.T, spread_y.reshape(72, 144))]
-    return (*two(rep), *two(fy), *two(fy.T), *two(fz), *two(fz.T), *exact)
+    pieces = {"ix": exact[0], "spread_y": exact[1]}
+    for name, table in (("fy", fy), ("gy", fy.T), ("fz", fz), ("gz", fz.T)):
+        pieces[name + "_h"], pieces[name + "_l"] = two(table)
+    by_span = rep.reshape(256, NY // 2, 256).transpose(1, 0, 2).reshape(-1, 256)
+    pieces["rep_h"], pieces["rep_l"] = two(by_span)
+    place, stack, row = {}, [], 0
+    for name, piece in pieces.items():
+        rows, columns = piece.shape
+        place[name] = (row, rows, columns)
+        stack.append(np.pad(piece, ((0, -rows % 16), (0, 256 - columns))))
+        row += rows + -rows % 16
+    return np.concatenate(stack, axis=0), place
 
 
 def split2(value):
@@ -111,18 +123,16 @@
 
 
 def kernel(
-    cell_in, offset_in, charge_in, width_in, coarse_in, density_in, history_in, *refs
+    place, cell_in, offset_in, charge_in, width_in, coarse_in, density_in, history_in, tables_in, *refs
 ):
-    tables_in, refs = refs[:12], refs[12:]
     residual_out, potential_out, sums_out = refs[:3]
     (
-        cell, offset, charge, width, coarse, density, history,
-        rep_h, rep_l, fy_h, fy_l, gy_h, gy_l, fz_h, fz_l, gz_h, gz_l, ix, spread_y,
+        cell, offset, charge, width, coarse, density, history, all_tables,
         planes, atoms, field_0, field_1, out_0, out_1, hist_0, hist_1,
-        send1, recv1, send2, recv2, send4, recv4, send5, recv5, send_h, recv_h,
+        send1, recv1, send2, recv2, send4, recv4, send5, recv5, send_g, recv_g, send_h, recv_h,
         weight, row_a, row_b,
         load_sem, halo_send, halo_recv, atom_send, atom_recv,
-        s1, r1, s2, r2, s4, r4, s5, r5, sh, rh, sa, ra, sb, rb, ring_z_ready, ring_y_ready, plane_ready,
+        s1, r1, s2, r2, s4, r4, s5, r5, sg, rg, sh, rh, sa, ra, sb, rb, ring_z_ready, ring_y_ready, plane_ready,
     ) = refs[3:]
     gz = lax.axis_index("gz")
     gy = lax.axis_index("gy")
@@ -146,18 +156,23 @@
         greet(barrier, z, y)
 
     sources = (
-        cell_in, offset_in, charge_in, width_in, coarse_in, density_in, tables_in[11], tables_in[10],
-        tables_in[0], tables_in[1], tables_in[2], tables_in[3], history_in,
-        *tables_in[4:10],
+        cell_in, offset_in, charge_in, width_in, coarse_in, density_in, tables_in, history_in,
     )
-    targets = (
-        cell, offset, charge, width, coarse, density, spread_y, ix,
-        rep_h, rep_l, fy_h, fy_l, history, gy_h, gy_l, fz_h, fz_l, gz_h, gz_l,
-    )
+    targets = (cell, offset, charge, width, coarse, density, all_tables, history)
     loads = {}
     for k, (source, target) in enumerate(zip(sources, targets)):
         loads[k] = pltpu.make_async_copy(source, target, load_sem.at[k])
         loads[k].start()
+
+    def table(name):
+        row, rows, columns = place[name]
+        return all_tables[row : row + rows, :columns]
+
+    def spans(p):
+        return tuple(
+            all_tables[place[name][0] + 256 * p : place[name][0] + 256 * p + 256, :]
+            for name in ("rep_h", "rep_l")
+        )
 
     row8 = lax.broadcasted_iota(jnp.int32, (8, 128), 0)
     lane8 = lax.broadcasted_iota(jnp.int32, (8, 128), 1)
@@ -198,6 +213,24 @@
         own = jnp.where(row8 == k, value, own)
     atoms[4] = own
 
+    pl.semaphore_wait(barrier, len(greeted))
+
+    neighbours = {}
+    for dz in (-1, 1, 0):
+        for dy in (-1, 1, 0):
+            if (dz, dy) != (0, 0):
+                slot = (1 - dz) * 3 + 1 - dy
+                neighbours[slot] = pltpu.make_async_remote_copy(
+                    atoms.at[4], atoms.at[slot], atom_send, atom_recv.at[2 * abs(dz) + abs(dy) - 1],
+                    device_id=zy(dz, dy), device_id_type=MESH,
+                )
+    for copy in neighbours.values():
+        copy.start()
+    for dy in (-4, 4):
+        greet(ring_z_ready, *zy(0, dy))
+    for dz in (-8, 8):
+        greet(ring_y_ready, *zy(dz, 0))
+
     plane_of = lax.broadcasted_iota(jnp.int32, (8, NC), 1)
     fine_of = lax.broadcasted_iota(jnp.int32, (8, NC), 0)
     away = plane_of - gz * (FZ // 2) - fine_of // 2
@@ -213,33 +246,16 @@
         parts = split3(coarse[k])
         planes[k] = dot(along_z, parts[0]) + dot(along_z, parts[1]) + dot(along_z, parts[2])
 
-    pl.semaphore_wait(barrier, len(greeted))
-
-    neighbours = {}
-    for dz in (-1, 1, 0):
-        for dy in (-1, 1, 0):
-            if (dz, dy) != (0, 0):
-                slot = (1 - dz) * 3 + 1 - dy
-                neighbours[slot] = pltpu.make_async_remote_copy(
-                    atoms.at[4], atoms.at[slot], atom_send.at[slot], atom_recv.at[slot],
-                    device_id=zy(dz, dy), device_id_type=MESH,
-                )
     own_planes = planes.at[pl.ds(0, 6)]
     halos = [
         pltpu.make_async_remote_copy(
-            own_planes, planes.at[pl.ds(6 * k, 6)], halo_send.at[k - 1], halo_recv.at[k - 1],
+            own_planes, planes.at[pl.ds(6 * k, 6)], halo_send, halo_recv,
             device_id=zy(0, dy), device_id_type=MESH,
         )
         for k, dy in ((1, 1), (2, -1))
     ]
-    for copy in neighbours.values():
-        copy.start()
     for copy in halos:
         copy.start()
-    for dy in (-4, 4):
-        greet(ring_z_ready, *zy(0, dy))
-    for dz in (-8, 8):
-        greet(ring_y_ready, *zy(dz, 0))
 
     lane128 = lax.broadcasted_iota(jnp.int32, (FZ, 128), 1)
     loads[5].wait()
@@ -295,82 +311,32 @@
         return [factor * jnp.maximum(power - floor, 0.0) for power in powers]
 
     total = charge_of(4)
-    for k in range(6, 12):
-        loads[k].wait()
-
-    for copy in halos:
-        copy.wait_recv()
-    parts = split3(planes[...].reshape(144, NC))
-    table = ix[...]
-    along_x = dot(parts[0], table) + dot(parts[1], table) + dot(parts[2], table)
-    parts = split3(along_x)
-    table = spread_y[...]
-    smooth = dot(table, parts[0]) + dot(table, parts[1]) + dot(table, parts[2])
-
-    for k in (3, 5, 1, 7, 0, 2, 6, 8):
-        neighbours[k].wait_recv()
-        total = [a + b for a, b in zip(total, charge_of(k))]
-
-    inside = lax.broadcasted_iota(jnp.int32, (8, 256), 1) < NF
-    blocks = []
-    for g in range(9):
-        rows = slice(8 * g, 8 * g + 8)
-        given = jnp.concatenate([field_0[rows, :], field_1[rows, :]], axis=1)
-        value = jnp.where(inside, smooth[rows] + total[g] - given, 0.0)
-        blocks.append(value)
-        field_0[rows, :] = value[:, :128]
-        field_1[rows, :] = value[:, 128:]
 
     group256 = double(group)
 
     def along_x_forward(values, store):
-        halves = split2(values)
+        count = values.shape[0]
+        high, low = split2(values)
+        both = jnp.concatenate([high, low], axis=0)
         for p in range(NY // 2):
-            span = slice(256 * p, 256 * p + 256)
-            out = dot3(halves, (rep_h[:, span], rep_l[:, span]))
-            chosen = out[0:8]
-            for g in range(1, 9):
-                chosen = jnp.where(group256 >= g, out[8 * g : 8 * g + 8], chosen)
-            store(2 * p, chosen[:, :128])
-            store(2 * p + 1, chosen[:, 128:])
-
-    def exchange_y(send, recv, ssem, rsem):
-        def act(j):
-            pltpu.make_async_remote_copy(
-                send.at[j], recv.at[gy], ssem, rsem, device_id=(gz, j), device_id_type=MESH
-            ).start()
-
-        each_partner(gy, NY, act)
-        recv[gy] = send[gy]
-        whole = recv.at[pl.ds(0, NY - 1)]
-        return pltpu.make_async_copy(whole, whole, rsem), pltpu.make_async_copy(whole, whole, ssem)
-
-    def exchange_z(send, recv, ssem, rsem):
-        mine = pl.ds(pl.multiple_of(gz * 8, 8), KY)
-
-        def act(j):
-            pltpu.make_async_remote_copy(
-                send.at[pl.ds(pl.multiple_of(j * 8, 8), KY)], recv.at[mine],
-                ssem, rsem, device_id=(j, gy), device_id_type=MESH,
-            ).start()
-
-        each_partner(gz, NZ, act)
-        recv[mine, :] = send[mine, :]
-        whole = recv.at[pl.ds(0, KY * (NZ - 1))]
-        return pltpu.make_async_copy(whole, whole, rsem), pltpu.make_async_copy(whole, whole, ssem)
-
-    def store_residual(j, value):
-        send1[j] = value
-
-    along_x_forward(jnp.concatenate(blocks, axis=0), store_residual)
-    pl.semaphore_wait(ring_z_ready, 2)
-    arrived, sent1 = exchange_y(send1, recv1, s1, r1)
-
-    pl.semaphore_wait(ring_y_ready, 2)
-    for j in ring_x:
-        greet(plane_ready, j, gy)
-
-    loads[12].wait()
+            rep_h, rep_l = spans(p)
+            out = dot(both, rep_h)
+            out = out[:count] + (out[count:] + dot(high, rep_l))
+            for i in range(count // 72):
+                chosen = out[72 * i : 72 * i + 8]
+                for g in range(1, 9):
+                    chosen = jnp.where(group256 >= g, out[72 * i + 8 * g : 72 * i + 8 * g + 8], chosen)
+                store(2 * p, i, chosen[:, :128])
+                store(2 * p + 1, i, chosen[:, 128:])
+
+    def history_along_x(first, count, send):
+        def store(j, i, value):
+            send[j, i] = value
+
+        rows = slice(72 * first, 72 * (first + count))
+        along_x_forward(jnp.concatenate([hist_0[rows, :], hist_1[rows, :]], axis=1), store)
+
+    loads[7].wait()
     lane_h = lax.broadcasted_iota(jnp.int32, (HIST, 128), 1)
     for c in range(FZ):
         for pair in range(FY // 2):
@@ -384,17 +350,70 @@
                 row = 8 * c + y if y < 8 else 48 + 8 * (c % 3) + 4 * (c // 3) + y - 8
                 hist_0[pl.ds(row, HIST, stride=72), :] = low
                 hist_1[pl.ds(row, HIST, stride=72), :] = high
-
-    def one_history(i, _):
-        rows = pl.ds(pl.multiple_of(i * 72, 8), 72)
-
-        def store(j, value):
-            send_h[j, i] = value
-
-        along_x_forward(jnp.concatenate([hist_0[rows, :], hist_1[rows, :]], axis=1), store)
-        return 0
-
-    lax.fori_loop(0, HIST, one_history, 0)
+    loads[6].wait()
+    history_along_x(0, EARLY, send_g)
+
+    whole = planes.at[pl.ds(0, 12)]
+    pltpu.make_async_copy(whole, whole, halo_recv).wait()
+    parts = split3(planes[...].reshape(144, NC))
+    weights = table("ix")
+    along_x = dot(parts[0], weights) + dot(parts[1], weights) + dot(parts[2], weights)
+    parts = split3(along_x)
+    weights = table("spread_y")
+    smooth = dot(weights, parts[0]) + dot(weights, parts[1]) + dot(weights, parts[2])
+
+    for kind, slots in ((0, (3, 5)), (1, (1, 7)), (2, (0, 2, 6, 8))):
+        whole = atoms.at[pl.ds(0, len(slots))]
+        pltpu.make_async_copy(whole, whole, atom_recv.at[kind]).wait()
+        for k in slots:
+            total = [a + b for a, b in zip(total, charge_of(k))]
+
+    inside = lax.broadcasted_iota(jnp.int32, (8, 256), 1) < NF
+    blocks = []
+    for g in range(9):
+        rows = slice(8 * g, 8 * g + 8)
+        given = jnp.concatenate([field_0[rows, :], field_1[rows, :]], axis=1)
+        value = jnp.where(inside, smooth[rows] + total[g] - given, 0.0)
+        blocks.append(value)
+        field_0[rows, :] = value[:, :128]
+        field_1[rows, :] = value[:, 128:]
+
+    def exchange_y(send, recv, ssem, rsem):
+        def act(j):
+            pltpu.make_async_remote_copy(
+                send.at[j], recv.at[gy], ssem, rsem, device_id=(gz, j), device_id_type=MESH
+            ).start()
+
+        each_partner(gy, NY, act)
+        recv[gy] = send[gy]
+        whole = recv.at[pl.ds(0, NY - 1)]
+        return pltpu.make_async_copy(whole, whole, rsem), pltpu.make_async_copy(whole, whole, ssem)
+
+    def exchange_z(send, recv, ssem, rsem):
+        mine = pl.ds(pl.multiple_of(gz * 8, 8), KY)
+
+        def act(j):
+            pltpu.make_async_remote_copy(
+                send.at[pl.ds(pl.multiple_of(j * 8, 8), KY)], recv.at[mine],
+                ssem, rsem, device_id=(j, gy), device_id_type=MESH,
+            ).start()
+
+        each_partner(gz, NZ, act)
+        recv[mine, :] = send[mine, :]
+        whole = recv.at[pl.ds(0, KY * (NZ - 1))]
+        return pltpu.make_async_copy(whole, whole, rsem), pltpu.make_async_copy(whole, whole, ssem)
+
+    def store_residual(j, i, value):
+        send1[j] = value
+
+    along_x_forward(jnp.concatenate(blocks, axis=0), store_residual)
+    pl.semaphore_wait(ring_z_ready, 2)
+    arrived, sent1 = exchange_y(send1, recv1, s1, r1)
+    arrived_g, sent_g = exchange_y(send_g, recv_g, sg, rg)
+    pl.semaphore_wait(ring_y_ready, 2)
+    for j in ring_x:
+        greet(plane_ready, j, gy)
+    history_along_x(EARLY, HIST - EARLY, send_h)
 
     groups128 = jnp.concatenate([group] * NY, axis=0)
     rows128 = jnp.concatenate([row8] * NY, axis=0)
@@ -405,7 +424,7 @@
     moved = jnp.where(
         from_upper, pltpu.roll(packed, 128 - 72, 1), jnp.where(from_lower, pltpu.roll(packed, 128 - 36, 1), 0.0)
     )
-    send2[...] = dot3((fy_h[...], fy_l[...]), split2(jnp.concatenate([packed, moved], axis=0)))
+    send2[...] = dot3((table("fy_h"), table("fy_l")), split2(jnp.concatenate([packed, moved], axis=0)))
     pl.semaphore_wait(plane_ready, 3)
     arrived, sent2 = exchange_z(send2, recv2, s2, r2)
     arrived_h, sent_h = exchange_y(send_h, recv_h, sh, rh)
@@ -427,8 +446,6 @@
                     out[top : top + count, 384 * pair + 128 * k : 384 * pair + 128 * k + 128] = tile
 
     give(residual_out, field_0, field_1)
-    for k in range(13, 19):
-        loads[k].wait()
     arrived.wait()
 
     group1 = group[0:1]
@@ -443,8 +460,8 @@
 
     pieces = [recv2[pl.ds(b, NZ, stride=8), :] for b in range(KY)]
     stacked = jnp.concatenate([swapped(pieces, a) for a in range(FZ)], axis=0)
-    spectrum = dot3((fz_h[...], fz_l[...]), split2(stacked)) * weight[...]
-    back = dot3((gz_h[...], gz_l[...]), split2(spectrum))
+    spectrum = dot3((table("fz_h"), table("fz_l")), split2(stacked)) * weight[...]
+    back = dot3((table("gz_h"), table("gz_l")), split2(spectrum))
     pieces = [back[NZ * a : NZ * a + NZ] for a in range(FZ)]
     for b in range(KY):
         send4[pl.ds(b, NZ, stride=8), :] = swapped(pieces, b)
@@ -452,17 +469,20 @@
     arrived.wait()
 
     rows256 = jnp.concatenate([rows128, rows128], axis=0)
-    out = dot3((gy_h[...], gy_l[...]), split2(jnp.where(rows256 < KY, recv4[0:256, :], 0.0)))
+    out = dot3((table("gy_h"), table("gy_l")), split2(jnp.where(rows256 < KY, recv4[0:256, :], 0.0)))
     low, high = out[:128], out[128:]
     packed = jnp.where(
         groups128 < 6, low, jnp.where(rows128 < 4, pltpu.roll(high, 72, 1), pltpu.roll(high, 36, 1))
     )
+    arrived_g.wait()
     arrived_h.wait()
     terms = [jnp.zeros((8, 128), F32) for _ in range(HIST + 1)]
     for j in range(NY):
         tile = jnp.where(group < 9, packed[8 * j : 8 * j + 8], 0.0)
-        for i in range(HIST):
-            terms[i] = terms[i] + recv_h[j, i] * tile
+        for i in range(EARLY):
+            terms[i] = terms[i] + recv_g[j, i] * tile
+        for i in range(EARLY, HIST):
+            terms[i] = terms[i] + recv_h[j, i - EARLY] * tile
         terms[HIST] = terms[HIST] + recv1[j] * tile
     rows = jnp.concatenate(
         [jnp.sum(t, axis=0, keepdims=True) for t in terms] + [jnp.zeros((7, 128), F32)], axis=0
@@ -502,8 +522,7 @@
             jnp.concatenate([jnp.where(group256 == g, part.astype(F32), 0.0) for g in range(9)], axis=0).astype(BF16)
             for part in pair
         ]
-        span = slice(256 * p, 256 * p + 256)
-        potential = potential + dot3(masked, (rep_h[:, span], rep_l[:, span]), dot_nt)
+        potential = potential + dot3(masked, spans(p), dot_nt)
     out_0[0:72, :] = potential[:, :128]
     out_1[0:72, :] = potential[:, 128:]
     give(potential_out, out_0, out_1)
@@ -512,11 +531,11 @@
     pltpu.make_async_copy(whole_a, whole_a, ra).wait()
     sums_out[...] = jnp.sum(row_a[...], axis=0)[0, : HIST + 1]
 
-    for copy in neighbours.values():
-        copy.wait_send()
-    for copy in halos:
-        copy.wait_send()
-    for copy in (sent1, sent2, sent_h, sent4, sent5):
+    whole = atoms.at[pl.ds(0, 8)]
+    pltpu.make_async_copy(whole, whole, atom_send).wait()
+    whole = planes.at[pl.ds(0, 12)]
+    pltpu.make_async_copy(whole, whole, halo_send).wait()
+    for copy in (sent1, sent2, sent_g, sent_h, sent4, sent5):
         copy.wait()
     pltpu.make_async_copy(whole_a, whole_a, sa).wait()
     pltpu.make_async_copy(whole_b, whole_b, sb).wait()
@@ -531,19 +550,19 @@
 
 
 def solution(mesh):
-    constants = tables()
+    constants, place = tables()
 
     def local(coarse, density, history, cell, offset, charge, width):
         coarse = jnp.transpose(coarse, (1, 0, 2))
         history = jnp.transpose(history, (1, 0, 2))
         offset = jnp.transpose(offset, (1, 2, 3, 0))
         inputs = (cell, offset, charge, width, coarse, density, history)
-        inputs = inputs + tuple(jnp.asarray(c) for c in constants)
+        inputs = (*inputs, jnp.asarray(constants))
         vmem = pl.BlockSpec(memory_space=pltpu.VMEM)
         dma = pltpu.SemaphoreType.DMA
         tile = (NY, 8, 128)
         residual, potential, sums = pl.pallas_call(
-            kernel,
+            functools.partial(kernel, place),
             out_shape=(
                 pltpu.VMEM((FZ, FY * NF), F32),
                 pltpu.VMEM((FZ, FY * NF), F32),
@@ -561,12 +580,13 @@
                 pltpu.VMEM((256, 128), F32),
                 *[pltpu.VMEM((264, 128), F32)] * 3,
                 *[pltpu.VMEM(tile, F32)] * 2,
-                *[pltpu.VMEM((NY, HIST, 8, 128), F32)] * 2,
+                *[pltpu.VMEM((NY, EARLY, 8, 128), F32)] * 2,
+                *[pltpu.VMEM((NY, HIST - EARLY, 8, 128), F32)] * 2,
                 pltpu.VMEM((NF, 128), F32),
                 pltpu.VMEM((NY, 1, 128), F32),
                 pltpu.VMEM((NZ, 1, 128), F32),
-                dma((19,)), dma((2,)), dma((2,)), dma((9,)), dma((9,)),
-                *[dma] * 14,
+                dma((8,)), dma, dma, dma, dma((3,)),
+                *[dma] * 16,
                 *[pltpu.SemaphoreType.REGULAR] * 3,
             ],
             compiler_params=pltpu.CompilerParams(collective_id=0, has_side_effects=True),

time: 53.3 us -> 52.4 us (0.983)
  Pallas kernels: 50.6 us -> 49.7 us
    pallas_call x1, Pallas kernels: 49.9 us -> 49 us  [local(): pl.pallas_call(functools.partial(kernel, place), out_shape=(pltpu.VMEM((F...]
where the time goes in v2:
time: 52.4 us; the launch traced here: 52.3 us
  Pallas kernels  49.7 us (95%)
  between operations  2.58 us (5%)
    pallas_call x1, Pallas kernels, local(): pl.pallas_call(functools.partial(kernel, place), out_shape=(pltpu.VMEM((F...  49 us

profile of v2, /device:TPU:1, one launch (start us, length us, event | category | flops | bytes accessed | tf_op | source)
XLA Modules:
  0.0 52.3 jit_solution(12354186427281904457)
XLA Ops:
  2.6 49.0 %shard_map.103 = (f32[6,2304]{1,0:T(8,128)S(1)}, f32[6,2304]{1,0:T(8,128)S(1)}, f32[9]{0:T(128)S(1)}) custom-call(s32[1,1,1]{2,1,0:T(1,128)S(6)} %copy.11.cell_in, f32[1,1,1,3]{3,2,1,0:T(1,128)} %bitcast.5, f32[1,1,1]{2,1,0:T(1,128)S(6)} %copy.12.charge_in, f32[1,1,1]{2,1,0:T(1,128)S(6)} %copy.13.width_in, f32[6,96,96]{2,1,0:T(8,128)} %bitcast.4, ...), custom_call_target="tpu_custom_call" | custom-call | tf_op jit(solution)/shard_map/pallas_call | solution.py:564
  51.6 0.7 %shard_map.104 = (f32[6,2304]{1,0:T(8,128)}, f32[6,2304]{1,0:T(8,128)}, f32[9]{0:T(128)}) custom-call(f32[6,2304]{1,0:T(8,128)S(1)} %get-tuple-element.6.refs_0_, f32[6,2304]{1,0:T(8,128)S(1)} %get-tuple-element.7.refs_1_, f32[9]{0:T(128)S(1)} %get-tuple-element.8.refs_2_), custom_call_target="tpu_custom_call" | custom-call | tf_op jit(solution)/shard_map/pallas_call | solution.py:596

commit v3 on v2

--- a/solution.py
+++ b/solution.py
@@ -107,6 +107,13 @@
     return product(a[0], b[0]) + product(a[1], b[0]) + product(a[0], b[1])
 
 
+def dot_data(table, value):
+    high, low = split2(value)
+    width = value.shape[1]
+    both = dot(table[0], jnp.concatenate([high, low], axis=1))
+    return both[:, :width] + (both[:, width:] + dot(table[1], high))
+
+
 def wrap(index, count):
     return jnp.where(index >= count, index - count, index)
 
@@ -403,17 +410,42 @@
         whole = recv.at[pl.ds(0, KY * (NZ - 1))]
         return pltpu.make_async_copy(whole, whole, rsem), pltpu.make_async_copy(whole, whole, ssem)
 
-    def store_residual(j, i, value):
-        send1[j] = value
-
-    along_x_forward(jnp.concatenate(blocks, axis=0), store_residual)
     pl.semaphore_wait(ring_z_ready, 2)
-    arrived, sent1 = exchange_y(send1, recv1, s1, r1)
+    high, low = split2(jnp.concatenate(blocks, axis=0))
+    both = jnp.concatenate([high, low], axis=0)
+    chip = gy // 2
+    for part in ((4, 3, 5), (2, 6, 1, 7, 0)):
+        done = []
+        for away in part:
+            p = wrap(chip + away, NY // 2)
+            rows = [
+                all_tables[pl.ds(pl.multiple_of(place[name][0] + 256 * p, 16), 256), :]
+                for name in ("rep_h", "rep_l")
+            ]
+            out = dot(both, rows[0])
+            out = out[:72] + (out[72:] + dot(high, rows[1]))
+            chosen = out[0:8]
+            for g in range(1, 9):
+                chosen = jnp.where(group256 >= g, out[8 * g : 8 * g + 8], chosen)
+            done.append((away, p, chosen))
+        for away, p, chosen in done:
+            send1[2 * p] = chosen[:, :128]
+            send1[2 * p + 1] = chosen[:, 128:]
+        for away, p, _ in done:
+            for j in (2 * p, 2 * p + 1) if away else (other_core,):
+                pltpu.make_async_remote_copy(
+                    send1.at[j], recv1.at[gy], s1, r1, device_id=(gz, j), device_id_type=MESH
+                ).start()
+    recv1[gy] = send1[gy]
+    whole = recv1.at[pl.ds(0, NY - 1)]
+    arrived = pltpu.make_async_copy(whole, whole, r1)
+    sent1 = pltpu.make_async_copy(whole, whole, s1)
     arrived_g, sent_g = exchange_y(send_g, recv_g, sg, rg)
     pl.semaphore_wait(ring_y_ready, 2)
     for j in ring_x:
         greet(plane_ready, j, gy)
     history_along_x(EARLY, HIST - EARLY, send_h)
+    arrived_h, sent_h = exchange_y(send_h, recv_h, sh, rh)
 
     groups128 = jnp.concatenate([group] * NY, axis=0)
     rows128 = jnp.concatenate([row8] * NY, axis=0)
@@ -424,10 +456,9 @@
     moved = jnp.where(
         from_upper, pltpu.roll(packed, 128 - 72, 1), jnp.where(from_lower, pltpu.roll(packed, 128 - 36, 1), 0.0)
     )
-    send2[...] = dot3((table("fy_h"), table("fy_l")), split2(jnp.concatenate([packed, moved], axis=0)))
+    send2[...] = dot_data((table("fy_h"), table("fy_l")), (jnp.concatenate([packed, moved], axis=0)))
     pl.semaphore_wait(plane_ready, 3)
     arrived, sent2 = exchange_z(send2, recv2, s2, r2)
-    arrived_h, sent_h = exchange_y(send_h, recv_h, sh, rh)
 
     def give(out, first, second):
         for pair in range(FY // 2):
@@ -460,8 +491,8 @@
 
     pieces = [recv2[pl.ds(b, NZ, stride=8), :] for b in range(KY)]
     stacked = jnp.concatenate([swapped(pieces, a) for a in range(FZ)], axis=0)
-    spectrum = dot3((table("fz_h"), table("fz_l")), split2(stacked)) * weight[...]
-    back = dot3((table("gz_h"), table("gz_l")), split2(spectrum))
+    spectrum = dot_data((table("fz_h"), table("fz_l")), (stacked)) * weight[...]
+    back = dot_data((table("gz_h"), table("gz_l")), (spectrum))
     pieces = [back[NZ * a : NZ * a + NZ] for a in range(FZ)]
     for b in range(KY):
         send4[pl.ds(b, NZ, stride=8), :] = swapped(pieces, b)
@@ -469,7 +500,7 @@
     arrived.wait()
 
     rows256 = jnp.concatenate([rows128, rows128], axis=0)
-    out = dot3((table("gy_h"), table("gy_l")), split2(jnp.where(rows256 < KY, recv4[0:256, :], 0.0)))
+    out = dot_data((table("gy_h"), table("gy_l")), (jnp.where(rows256 < KY, recv4[0:256, :], 0.0)))
     low, high = out[:128], out[128:]
     packed = jnp.where(
         groups128 < 6, low, jnp.where(rows128 < 4, pltpu.roll(high, 72, 1), pltpu.roll(high, 36, 1))
@@ -527,18 +558,17 @@
     out_1[0:72, :] = potential[:, 128:]
     give(potential_out, out_0, out_1)
 
-    whole_a = row_a.at[pl.ds(0, NY - 1)]
-    pltpu.make_async_copy(whole_a, whole_a, ra).wait()
-    sums_out[...] = jnp.sum(row_a[...], axis=0)[0, : HIST + 1]
-
     whole = atoms.at[pl.ds(0, 8)]
     pltpu.make_async_copy(whole, whole, atom_send).wait()
     whole = planes.at[pl.ds(0, 12)]
     pltpu.make_async_copy(whole, whole, halo_send).wait()
     for copy in (sent1, sent2, sent_g, sent_h, sent4, sent5):
         copy.wait()
+    pltpu.make_async_copy(whole_b, whole_b, sb).wait()
+    whole_a = row_a.at[pl.ds(0, NY - 1)]
     pltpu.make_async_copy(whole_a, whole_a, sa).wait()
-    pltpu.make_async_copy(whole_b, whole_b, sb).wait()
+    pltpu.make_async_copy(whole_a, whole_a, ra).wait()
+    sums_out[...] = jnp.sum(row_a[...], axis=0)[0, : HIST + 1]
 
 
 def write_out(*refs):

time: 52.4 us -> 52 us (level)
  no operation moved by 1% of the time
where the time goes in v3:
time: 52 us; the launch traced here: 51.8 us
  Pallas kernels  49.2 us (95%)
  between operations  2.58 us (5%)
    pallas_call x1, Pallas kernels, local(): pl.pallas_call(functools.partial(kernel, place), out_shape=(pltpu.VMEM((F...  48.5 us

profile of v3, /device:TPU:1, one launch (start us, length us, event | category | flops | bytes accessed | tf_op | source)
XLA Modules:
  0.0 51.8 jit_solution(1027633045544722859)
XLA Ops:
  2.6 48.5 %shard_map.103 = (f32[6,2304]{1,0:T(8,128)S(1)}, f32[6,2304]{1,0:T(8,128)S(1)}, f32[9]{0:T(128)S(1)}) custom-call(s32[1,1,1]{2,1,0:T(1,128)S(6)} %copy.11.cell_in, f32[1,1,1,3]{3,2,1,0:T(1,128)} %bitcast.5, f32[1,1,1]{2,1,0:T(1,128)S(6)} %copy.12.charge_in, f32[1,1,1]{2,1,0:T(1,128)S(6)} %copy.13.width_in, f32[6,96,96]{2,1,0:T(8,128)} %bitcast.4, ...), custom_call_target="tpu_custom_call" | custom-call | tf_op jit(solution)/shard_map/pallas_call | solution.py:594
  51.1 0.7 %shard_map.104 = (f32[6,2304]{1,0:T(8,128)}, f32[6,2304]{1,0:T(8,128)}, f32[9]{0:T(128)}) custom-call(f32[6,2304]{1,0:T(8,128)S(1)} %get-tuple-element.6.refs_0_, f32[6,2304]{1,0:T(8,128)S(1)} %get-tuple-element.7.refs_1_, f32[9]{0:T(128)S(1)} %get-tuple-element.8.refs_2_), custom_call_target="tpu_custom_call" | custom-call | tf_op jit(solution)/shard_map/pallas_call | solution.py:626

commit v4 on v3

--- a/solution.py
+++ b/solution.py
@@ -45,10 +45,8 @@
             rep[:NF, j, g * KX : (g + 1) * KX] = h[:, j * KX : (j + 1) * KX]
     rep = rep.reshape(256, NY * 128)
     by_y = h.reshape(NZ, KY, NY, FY)
-    fy = np.zeros((NZ, 8, 2, NY, 8))
-    fy[:, :KY, 0] = by_y[:, :, :, :8]
-    fy[:, :KY, 1, :, :4] = by_y[:, :, :, 8:]
-    fy[:, :KY, 1, :, 4:] = by_y[:, :, :, 8:]
+    by_y = np.stack([by_y[:, :4], by_y[:, [4, 4, 5, 5]]])
+    fy = np.stack([by_y[..., :8], by_y[..., [8, 9, 10, 11, 8, 9, 10, 11]]], axis=3)
     fy = fy.reshape(256, 256)
     fz = h.reshape(NF, NZ, FZ).transpose(0, 2, 1).reshape(NF, NF)
     ix = np.zeros((256, NC))
@@ -397,17 +395,17 @@
         return pltpu.make_async_copy(whole, whole, rsem), pltpu.make_async_copy(whole, whole, ssem)
 
     def exchange_z(send, recv, ssem, rsem):
-        mine = pl.ds(pl.multiple_of(gz * 8, 8), KY)
+        mine = pl.ds(pl.multiple_of(gz * 4, 4), 4)
 
         def act(j):
             pltpu.make_async_remote_copy(
-                send.at[pl.ds(pl.multiple_of(j * 8, 8), KY)], recv.at[mine],
+                send.at[pl.ds(pl.multiple_of(j * 4, 4), 4)], recv.at[mine],
                 ssem, rsem, device_id=(j, gy), device_id_type=MESH,
             ).start()
 
         each_partner(gz, NZ, act)
         recv[mine, :] = send[mine, :]
-        whole = recv.at[pl.ds(0, KY * (NZ - 1))]
+        whole = recv.at[pl.ds(0, 4 * (NZ - 1))]
         return pltpu.make_async_copy(whole, whole, rsem), pltpu.make_async_copy(whole, whole, ssem)
 
     pl.semaphore_wait(ring_z_ready, 2)
@@ -456,7 +454,12 @@
     moved = jnp.where(
         from_upper, pltpu.roll(packed, 128 - 72, 1), jnp.where(from_lower, pltpu.roll(packed, 128 - 36, 1), 0.0)
     )
-    send2[...] = dot_data((table("fy_h"), table("fy_l")), (jnp.concatenate([packed, moved], axis=0)))
+    even_rows = rows128 % 2 == 0
+    out = dot_data((table("fy_h"), table("fy_l")), jnp.concatenate([packed, moved], axis=0))
+    high = out[128:]
+    send2[0:128, :] = jnp.where(
+        groups128 < 6, out[:128], jnp.where(even_rows, pltpu.roll(high, 72, 1), pltpu.roll(high, 36, 1))
+    )
     pl.semaphore_wait(plane_ready, 3)
     arrived, sent2 = exchange_z(send2, recv2, s2, r2)
 
@@ -489,18 +492,28 @@
             result = moved if result is None else jnp.where(group1 >= b, moved, result)
         return result
 
-    pieces = [recv2[pl.ds(b, NZ, stride=8), :] for b in range(KY)]
+    packed_rows = [recv2[pl.ds(r, NZ, stride=4), :] for r in range(4)]
+    pieces = packed_rows + [
+        jnp.where(group1 < 3, pltpu.roll(packed_rows[r], 128 - 72, 1), pltpu.roll(packed_rows[r + 1], 128 - 36, 1))
+        for r in (0, 2)
+    ]
     stacked = jnp.concatenate([swapped(pieces, a) for a in range(FZ)], axis=0)
     spectrum = dot_data((table("fz_h"), table("fz_l")), (stacked)) * weight[...]
     back = dot_data((table("gz_h"), table("gz_l")), (spectrum))
     pieces = [back[NZ * a : NZ * a + NZ] for a in range(FZ)]
-    for b in range(KY):
-        send4[pl.ds(b, NZ, stride=8), :] = swapped(pieces, b)
+    pieces = [swapped(pieces, b) for b in range(KY)]
+    for r in range(4):
+        beside = pltpu.roll(pieces[4 + r // 2], 36 if r % 2 else 72, 1)
+        send4[pl.ds(r, NZ, stride=4), :] = jnp.where(group1 < 6, pieces[r], beside)
     arrived, sent4 = exchange_z(send4, recv4, s4, r4)
     arrived.wait()
 
-    rows256 = jnp.concatenate([rows128, rows128], axis=0)
-    out = dot_data((table("gy_h"), table("gy_l")), (jnp.where(rows256 < KY, recv4[0:256, :], 0.0)))
+    packed = recv4[0:128, :]
+    moved = jnp.where(
+        even_rows & (groups128 < 3), pltpu.roll(packed, 128 - 72, 1),
+        jnp.where((rows128 % 2 == 1) & (groups128 >= 3) & (groups128 < 6), pltpu.roll(packed, 128 - 36, 1), 0.0),
+    )
+    out = dot_data((table("gy_h"), table("gy_l")), jnp.concatenate([packed, moved], axis=0))
     low, high = out[:128], out[128:]
     packed = jnp.where(
         groups128 < 6, low, jnp.where(rows128 < 4, pltpu.roll(high, 72, 1), pltpu.roll(high, 36, 1))
@@ -607,8 +620,7 @@
                 *[pltpu.VMEM((128, 128), F32)] * 4,
                 *[pltpu.VMEM((648, 128), F32)] * 2,
                 *[pltpu.VMEM(tile, F32)] * 2,
-                pltpu.VMEM((256, 128), F32),
-                *[pltpu.VMEM((264, 128), F32)] * 3,
+                *[pltpu.VMEM((136, 128), F32)] * 4,
                 *[pltpu.VMEM(tile, F32)] * 2,
                 *[pltpu.VMEM((NY, EARLY, 8, 128), F32)] * 2,
                 *[pltpu.VMEM((NY, HIST - EARLY, 8, 128), F32)] * 2,

time: 52 us -> 51.6 us (level)
  no operation moved by 1% of the time
where the time goes in v4:
time: 51.6 us; the launch traced here: 51.4 us
  Pallas kernels  48.8 us (95%)
  between operations  2.58 us (5%)
    pallas_call x1, Pallas kernels, local(): pl.pallas_call(functools.partial(kernel, place), out_shape=(pltpu.VMEM((F...  48.2 us

profile of v4, /device:TPU:1, one launch (start us, length us, event | category | flops | bytes accessed | tf_op | source)
XLA Modules:
  0.0 51.4 jit_solution(5039530973703790904)
XLA Ops:
  2.6 48.2 %shard_map.103 = (f32[6,2304]{1,0:T(8,128)S(1)}, f32[6,2304]{1,0:T(8,128)S(1)}, f32[9]{0:T(128)S(1)}) custom-call(s32[1,1,1]{2,1,0:T(1,128)S(6)} %copy.11.cell_in, f32[1,1,1,3]{3,2,1,0:T(1,128)} %bitcast.5, f32[1,1,1]{2,1,0:T(1,128)S(6)} %copy.12.charge_in, f32[1,1,1]{2,1,0:T(1,128)S(6)} %copy.13.width_in, f32[6,96,96]{2,1,0:T(8,128)} %bitcast.4, ...), custom_call_target="tpu_custom_call" | custom-call | tf_op jit(solution)/shard_map/pallas_call | solution.py:607
  50.7 0.7 %shard_map.104 = (f32[6,2304]{1,0:T(8,128)}, f32[6,2304]{1,0:T(8,128)}, f32[9]{0:T(128)}) custom-call(f32[6,2304]{1,0:T(8,128)S(1)} %get-tuple-element.6.refs_0_, f32[6,2304]{1,0:T(8,128)S(1)} %get-tuple-element.7.refs_1_, f32[9]{0:T(128)S(1)} %get-tuple-element.8.refs_2_), custom_call_target="tpu_custom_call" | custom-call | tf_op jit(solution)/shard_map/pallas_call | solution.py:638

commit v5 on v4

--- a/solution.py
+++ b/solution.py
@@ -135,7 +135,7 @@
         cell, offset, charge, width, coarse, density, history, all_tables,
         planes, atoms, field_0, field_1, out_0, out_1, hist_0, hist_1,
         send1, recv1, send2, recv2, send4, recv4, send5, recv5, send_g, recv_g, send_h, recv_h,
-        weight, row_a, row_b,
+        weight, row_a, row_b, hist_y,
         load_sem, halo_send, halo_recv, atom_send, atom_recv,
         s1, r1, s2, r2, s4, r4, s5, r5, sg, rg, sh, rh, sa, ra, sb, rb, ring_z_ready, ring_y_ready, plane_ready,
     ) = refs[3:]
@@ -449,17 +449,20 @@
     rows128 = jnp.concatenate([row8] * NY, axis=0)
     from_upper = (groups128 < 3) & (rows128 < 4)
     from_lower = (groups128 >= 3) & (groups128 < 6) & (rows128 >= 4)
+    even_rows = rows128 % 2 == 0
+
+    def along_y_forward(packed):
+        moved = jnp.where(
+            from_upper, pltpu.roll(packed, 128 - 72, 1), jnp.where(from_lower, pltpu.roll(packed, 128 - 36, 1), 0.0)
+        )
+        out = dot_data((table("fy_h"), table("fy_l")), jnp.concatenate([packed, moved], axis=0))
+        high = out[128:]
+        return jnp.where(
+            groups128 < 6, out[:128], jnp.where(even_rows, pltpu.roll(high, 72, 1), pltpu.roll(high, 36, 1))
+        )
+
     arrived.wait()
-    packed = recv1[...].reshape(128, 128)
-    moved = jnp.where(
-        from_upper, pltpu.roll(packed, 128 - 72, 1), jnp.where(from_lower, pltpu.roll(packed, 128 - 36, 1), 0.0)
-    )
-    even_rows = rows128 % 2 == 0
-    out = dot_data((table("fy_h"), table("fy_l")), jnp.concatenate([packed, moved], axis=0))
-    high = out[128:]
-    send2[0:128, :] = jnp.where(
-        groups128 < 6, out[:128], jnp.where(even_rows, pltpu.roll(high, 72, 1), pltpu.roll(high, 36, 1))
-    )
+    send2[0:128, :] = along_y_forward(recv1[...].reshape(128, 128))
     pl.semaphore_wait(plane_ready, 3)
     arrived, sent2 = exchange_z(send2, recv2, s2, r2)
 
@@ -506,7 +509,40 @@
         beside = pltpu.roll(pieces[4 + r // 2], 36 if r % 2 else 72, 1)
         send4[pl.ds(r, NZ, stride=4), :] = jnp.where(group1 < 6, pieces[r], beside)
     arrived, sent4 = exchange_z(send4, recv4, s4, r4)
+
+    for first, count, part, here in ((0, EARLY, recv_g, arrived_g), (EARLY, HIST - EARLY, recv_h, arrived_h)):
+        here.wait()
+
+        def one_history(i, _, first=first, part=part):
+            hist_y[first + i] = along_y_forward(part[:, i].reshape(128, 128))
+            return 0
+
+        lax.fori_loop(0, count, one_history, 0, unroll=True)
+
     arrived.wait()
+    terms = [jnp.zeros((8, 128), F32) for _ in range(HIST + 1)]
+    for j in range(NY):
+        span = slice(8 * j, 8 * j + 8)
+        tile = jnp.where(group < 9, recv4[span, :], 0.0)
+        for i in range(HIST):
+            terms[i] = terms[i] + hist_y[i, span, :] * tile
+        terms[HIST] = terms[HIST] + send2[span, :] * tile
+    rows = jnp.concatenate(
+        [jnp.sum(t, axis=0, keepdims=True) for t in terms] + [jnp.zeros((7, 128), F32)], axis=0
+    ) * (1.0 / float(NF) ** 3)
+    column = jnp.sum(rows, axis=1, keepdims=True)
+    lane_of = lax.broadcasted_iota(jnp.int32, (16, 128), 1)
+    row_of = lax.broadcasted_iota(jnp.int32, (16, 128), 0)
+    line = jnp.sum(jnp.where(lane_of == row_of, column, 0.0), axis=0, keepdims=True)
+
+    row_b[gz] = line
+
+    def act_b(j):
+        pltpu.make_async_remote_copy(
+            row_b.at[gz], row_b.at[gz], sb, rb, device_id=(j, gy), device_id_type=MESH
+        ).start()
+
+    each_partner(gz, NZ, act_b)
 
     packed = recv4[0:128, :]
     moved = jnp.where(
@@ -518,32 +554,6 @@
     packed = jnp.where(
         groups128 < 6, low, jnp.where(rows128 < 4, pltpu.roll(high, 72, 1), pltpu.roll(high, 36, 1))
     )
-    arrived_g.wait()
-    arrived_h.wait()
-    terms = [jnp.zeros((8, 128), F32) for _ in range(HIST + 1)]
-    for j in range(NY):
-        tile = jnp.where(group < 9, packed[8 * j : 8 * j + 8], 0.0)
-        for i in range(EARLY):
-            terms[i] = terms[i] + recv_g[j, i] * tile
-        for i in range(EARLY, HIST):
-            terms[i] = terms[i] + recv_h[j, i - EARLY] * tile
-        terms[HIST] = terms[HIST] + recv1[j] * tile
-    rows = jnp.concatenate(
-        [jnp.sum(t, axis=0, keepdims=True) for t in terms] + [jnp.zeros((7, 128), F32)], axis=0
-    ) * (1.0 / float(NF) ** 3)
-    column = jnp.sum(rows, axis=1, keepdims=True)
-    lane_of = lax.broadcasted_iota(jnp.int32, (16, 128), 1)
-    row_of = lax.broadcasted_iota(jnp.int32, (16, 128), 0)
-    line = jnp.sum(jnp.where(lane_of == row_of, column, 0.0), axis=0, keepdims=True)
-
-    row_b[gz] = line
-
-    def act_b(j):
-        pltpu.make_async_remote_copy(
-            row_b.at[gz], row_b.at[gz], sb, rb, device_id=(j, gy), device_id_type=MESH
-        ).start()
-
-    each_partner(gz, NZ, act_b)
     for j in range(NY):
         send5[j] = packed[8 * j : 8 * j + 8]
     arrived, sent5 = exchange_y(send5, recv5, s5, r5)
@@ -627,6 +637,7 @@
                 pltpu.VMEM((NF, 128), F32),
                 pltpu.VMEM((NY, 1, 128), F32),
                 pltpu.VMEM((NZ, 1, 128), F32),
+                pltpu.VMEM((HIST, 128, 128), F32),
                 dma((8,)), dma, dma, dma, dma((3,)),
                 *[dma] * 16,
                 *[pltpu.SemaphoreType.REGULAR] * 3,

time: 51.6 us -> 51.2 us (level)
  no operation moved by 1% of the time
where the time goes in v5:
time: 51.2 us; the launch traced here: 51 us
  Pallas kernels  48.5 us (95%)
  between operations  2.58 us (5%)
    pallas_call x1, Pallas kernels, local(): pl.pallas_call(functools.partial(kernel, place), out_shape=(pltpu.VMEM((F...  47.8 us

profile of v5, /device:TPU:1, one launch (start us, length us, event | category | flops | bytes accessed | tf_op | source)
XLA Modules:
  0.0 51.0 jit_solution(7575709825449191303)
XLA Ops:
  2.6 47.8 %shard_map.103 = (f32[6,2304]{1,0:T(8,128)S(1)}, f32[6,2304]{1,0:T(8,128)S(1)}, f32[9]{0:T(128)S(1)}) custom-call(s32[1,1,1]{2,1,0:T(1,128)S(6)} %copy.11.cell_in, f32[1,1,1,3]{3,2,1,0:T(1,128)} %bitcast.5, f32[1,1,1]{2,1,0:T(1,128)S(6)} %copy.12.charge_in, f32[1,1,1]{2,1,0:T(1,128)S(6)} %copy.13.width_in, f32[6,96,96]{2,1,0:T(8,128)} %bitcast.4, ...), custom_call_target="tpu_custom_call" | custom-call | tf_op jit(solution)/shard_map/pallas_call | solution.py:617
  50.4 0.7 %shard_map.104 = (f32[6,2304]{1,0:T(8,128)}, f32[6,2304]{1,0:T(8,128)}, f32[9]{0:T(128)}) custom-call(f32[6,2304]{1,0:T(8,128)S(1)} %get-tuple-element.6.refs_0_, f32[6,2304]{1,0:T(8,128)S(1)} %get-tuple-element.7.refs_1_, f32[9]{0:T(128)S(1)} %get-tuple-element.8.refs_2_), custom_call_target="tpu_custom_call" | custom-call | tf_op jit(solution)/shard_map/pallas_call | solution.py:649
